TPU v7x, 32 devices: a whole 2x2x4 slice. The times are simulated.
32 devices in a mesh: section: 2 (over x), blk: 8 (over z, y), head: 2 (over core).
Axes of the slice: x: 2, y: 2, z: 4, core: 2. Of those that a mesh axis runs over, the one named last changes fastest.
Arguments:
- hidden_in: bfloat16 [4, 64, 1536], P(None, 'blk', 'head'), may hold values from -6 to 6
- w_qkv: bfloat16 [2, 1536, 3, 1536], P('section', 'blk', None, 'head'), may hold values from -0.15625 to 0.15625
- norm_gain: float32 [2, 1536], P('section'), may hold values from 0.5 to 1.5
- qk_gain: float32 [2, 2, 128], P('section'), may hold values from 1 to 2
- text_states: bfloat16 [2, 256, 1536], P('section'), may hold values from -6 to 6
- text_len: int32 [1], replicated, may hold values from 64 to 256
- patch_len: int32 [4], replicated, may hold values from 32 to 64
- stale_flags: int32 [4, 2], replicated, may hold values from 0 to 1, as said below
- stale_kv: bfloat16 [2, 2, 4, 64, 1536], P('section', None, None, 'blk', 'head'), may hold values from -6 to 6
Outputs:
- hidden_out: bfloat16 [2, 4, 64, 1536], P('section', None, 'blk', 'head')
- new_cache: bfloat16 [2, 2, 4, 64, 1536], P('section', None, None, 'blk', 'head')
Inputs may be any that keep to these rules, and one draw needn't show every extreme that they name: `stale_flags`: 1 means that the micro-batch uses the previous step's keys and values at that layer, 0 that it uses its fresh ones; every layer has at least one micro-batch flagged 1 and at least one flagged 0.
All inputs are finite; a program needn't handle non-finite values.
Results may differ from a plain program's by a relative error of at most 0.02.
Values may be sent and summed in bfloat16 or wider, within the bound.
A program may use at most 64 MiB of HBM per device.

v0:
```python
import functools

import jax
import jax.numpy as jnp
from jax import lax
from jax.experimental import pallas as pl
from jax.experimental.pallas import tpu as pltpu
from jax.sharding import PartitionSpec as P

MESH = pl.DeviceIdType.MESH
F32 = jnp.float32
BF16 = jnp.bfloat16


def rms(values, gain):
    return values * lax.rsqrt(jnp.mean(values * values, axis=-1, keepdims=True) + 1e-06) * gain


def kernel(
    dims,
    text_len, patch_len, flags,
    hid_in, w_in, row_gain, head_gain, text_hbm, stale_in,
    hid_out, cache_out,
    X, X1, RES, G, XN, text_in, TN, W, ST, TK, TV, hid_own, cache_own,
    zs, zr, ys, yr, ws, wr, ss, sr, hs, hr, cs, cr, gzs, gzr, gys, gyr, gxs, one,
):
    S, B, heads, hd, micro, tok = dims
    off = (B - heads) // 2
    rows = micro * tok
    total = B * rows
    width = heads * hd
    depth = w_in.shape[1]
    s, b, h = lax.axis_index("section"), lax.axis_index("blk"), lax.axis_index("head")
    mate = b + 1 - 2 * lax.rem(b, 2)
    j_own = b - off
    owner = (b >= off) & (b < off + heads)
    half = pl.ds(pl.multiple_of(h * width, hd), width)
    other_half = pl.ds(pl.multiple_of((1 - h) * width, hd), width)

    def ahead(k):
        return lax.rem(b + k, B)

    def remote(src, dst, send, recv, dev):
        return pltpu.make_async_remote_copy(
            src_ref=src, dst_ref=dst, send_sem=send, recv_sem=recv, device_id=dev, device_id_type=MESH
        )

    def arrived(dst, sem):
        pltpu.make_async_copy(dst, dst, sem).wait()

    def push(src, dst, send, recv, target):
        @pl.when(target == b)
        def _():
            pltpu.make_async_copy(src, dst, recv).start()

        @pl.when(target != b)
        def _():
            remote(src, dst, send, recv, (s, target, h)).start()

    def pushed(src, send, target):
        @pl.when(target != b)
        def _():
            remote(src, src, send, send, (s, target, h)).wait_send()

    text_copy = pltpu.make_async_copy(text_hbm, text_in, one.at[5])
    text_copy.start()
    barrier = pltpu.get_barrier_semaphore()
    for k in range(1, B):
        pl.semaphore_signal(barrier, inc=1, device_id=(s, ahead(k), h), device_id_type=MESH)
    pl.semaphore_signal(barrier, inc=1, device_id=(s, b, 1 - h), device_id_type=MESH)

    @pl.when(s > 0)
    def _():
        for k in range(0, B, 2):
            pl.semaphore_signal(barrier, inc=1, device_id=(s - 1, ahead(k), h), device_id_type=MESH)

    @pl.when(s < S - 1)
    def _():
        for k in range(0, B, 2):
            pl.semaphore_signal(barrier, inc=1, device_id=(s + 1, ahead(k), h), device_id_type=MESH)

    linked = (s > 0).astype(jnp.int32) + (s < S - 1).astype(jnp.int32)
    pl.semaphore_wait(barrier, B + linked * (B // 2))

    def row_block(c):
        return X.at[c, :, half]

    def col_block(j):
        return X1.at[h, j]

    def swap_cores():
        return remote(X.at[:, :, half], X.at[:, :, half], one.at[0], one.at[1], (s, b, 1 - h))

    def swap_blocks():
        return remote(X1.at[h], X1.at[h], one.at[0], one.at[1], (s, b, 1 - h))

    @pl.when(s == 0)
    def _():
        pltpu.make_async_copy(hid_in, row_block(b), one.at[2]).start()

    @pl.when(s == 1)
    def _():
        for k in range(2, B, 2):
            remote(hid_in, G.at[b], gzs.at[k], gzr.at[b], (s, ahead(k), h)).start()
        remote(hid_in, G.at[b], gys.at[0], gyr.at[b], (s, mate, h)).start()

    def hand_over(c, k):
        remote(G.at[c], row_block(c), gxs.at[k], yr.at[c], (s - 1, b, h)).start()

    @pl.when(s == 1)
    def _():
        for k in range(2, B, 2):
            c = ahead(k)
            arrived(G.at[c], gzr.at[c])
            remote(G.at[c], G.at[c], gys.at[k], gyr.at[c], (s, mate, h)).start()
            hand_over(c, k)

    w_dst = W.at[:, pl.ds(pl.multiple_of(b * depth, depth), depth), :]
    st_dst = ST.at[:, b]

    def cols_of(j):
        return pl.ds(pl.multiple_of(j * hd, hd), hd)

    for k in range(heads):
        j = lax.rem(b + k, heads)
        push(w_in.at[:, :, cols_of(j)], w_dst, ws.at[k], wr.at[b], j + off)
    for k in range(heads):
        j = lax.rem(b + k, heads)
        push(stale_in.at[:, :, cols_of(j)], st_dst, ss.at[k], sr.at[b], j + off)

    @pl.when(s == 1)
    def _():
        for k in range(0, B, 2):
            c = lax.rem(mate + k, B)
            arrived(G.at[c], gyr.at[c])
            hand_over(c, k + 1)

    def norm_states(values):
        values = values.astype(F32)
        XN[...] = rms(values, row_gain[...]).astype(BF16)

    @pl.when(s == 0)
    def _():
        pltpu.make_async_copy(hid_in, row_block(b), one.at[2]).wait()
        for k in range(1, B):
            arrived(row_block(ahead(k)), yr.at[ahead(k)])
        swap_cores().start()
        arrived(X.at[:, :, other_half], one.at[1])

        @pl.when(owner)
        def _():
            norm_states(X[...].reshape(total, 2 * width))
            RES[...] = X[:, :, pl.ds(pl.multiple_of(h * width + j_own * hd, hd), hd)].reshape(total, hd)

    text_copy.wait()

    @pl.when(owner)
    def _():
        TN[...] = rms(text_in[...].astype(F32), row_gain[...]).astype(BF16)
        for c in range(B):
            arrived(W.at[:, pl.ds(c * depth, depth), :], wr.at[c])
        text_kv = jnp.dot(
            TN[...], jnp.concatenate([W[1], W[2]], axis=1), preferred_element_type=F32
        ).astype(BF16)
        TK[...] = rms(text_kv[:, :hd].astype(F32), head_gain[1:2, :]).astype(BF16)
        TV[...] = text_kv[:, hd:]

    @pl.when(s > 0)
    def _():
        @pl.when(owner)
        def _():
            mine = col_block(j_own)
            arrived(mine, one.at[3])
            remote(mine, mine, ys.at[0], yr.at[b], (s, mate, h)).start()

        for k in range(2, B, 2):
            c = ahead(k)

            @pl.when((c >= off) & (c < off + heads))
            def _():
                block = col_block(c - off)
                arrived(block, zr.at[c])
                remote(block, block, ys.at[k], yr.at[c], (s, mate, h)).start()

        for k in range(0, B, 2):
            c = lax.rem(mate + k, B)

            @pl.when((c >= off) & (c < off + heads))
            def _():
                arrived(col_block(c - off), yr.at[c])

        swap_blocks().start()
        arrived(X1.at[1 - h], one.at[1])

        @pl.when(owner)
        def _():
            norm_states(
                jnp.concatenate([X1[i, j] for i in range(2) for j in range(heads)], axis=1)
            )
            RES[...] = X1[h, j_own]

    @pl.when(owner)
    def _():
        proj = jnp.dot(
            XN[...], jnp.concatenate([W[0], W[1], W[2]], axis=1), preferred_element_type=F32
        )
        fresh_k = proj[:, hd : 2 * hd].astype(BF16)
        fresh_v = proj[:, 2 * hd :].astype(BF16)
        cache_own[0] = fresh_k.reshape(B, rows, hd)
        cache_own[1] = fresh_v.reshape(B, rows, hd)
        cols = cols_of(j_own)
        for k in range(B):
            t = ahead(k)
            push(cache_own.at[:, t], cache_out.at[:, :, cols], cs.at[k], cr.at[j_own], t)
        for c in range(B):
            arrived(ST.at[:, c], sr.at[c])
        tok_bits = tok.bit_length() - 1

        def place(shape, axis):
            at = lax.broadcasted_iota(jnp.int32, shape, axis)
            which = lax.shift_right_logical(at, tok_bits) & (micro - 1)
            spot = lax.shift_right_logical(at, rows.bit_length() - 1) * tok + (at & (tok - 1))
            return which, spot

        def per_micro(which, read):
            out = jnp.zeros(which.shape, jnp.int32)
            for m in range(micro):
                out = jnp.where(which == m, read(m), out)
            return out

        which, _ = place((total, hd), 0)
        use_stale = per_micro(which, lambda m: flags[s, m]) == 1
        kept_k = jnp.where(use_stale, ST[0].reshape(total, hd).astype(F32), fresh_k.astype(F32))
        kept_v = jnp.where(use_stale, ST[1].reshape(total, hd).astype(F32), fresh_v.astype(F32))
        keys = rms(kept_k, head_gain[1:2, :]).astype(BF16)
        queries = rms(proj[:, :hd], head_gain[0:1, :]).astype(BF16)
        scale = hd**-0.5
        nt = (((1,), (1,)), ((), ()))

        def attend(key_rows, value_rows, mask):
            scores = lax.dot_general(queries, key_rows, nt, preferred_element_type=F32) * scale
            probs = jnp.where(mask, jnp.exp(scores), 0.0)
            num = jnp.dot(probs.astype(BF16), value_rows, preferred_element_type=F32)
            return num, jnp.sum(probs, axis=1, keepdims=True)

        shape = (total, total)
        q_which, _ = place(shape, 0)
        k_which, k_spot = place(shape, 1)
        mask = (q_which == k_which) & (k_spot < per_micro(k_which, lambda m: patch_len[m]))
        num, den = attend(keys, kept_v.astype(BF16), mask)
        text_at = lax.broadcasted_iota(jnp.int32, (total, TK.shape[0]), 1)
        text_num, text_den = attend(TK[...], TV[...], text_at < text_len[0])
        attended = (num + text_num) / (den + text_den)
        hid_own[...] = (RES[...].astype(F32) + attended).astype(BF16)

        @pl.when(s < S - 1)
        def _():
            remote(hid_own, col_block(j_own), one.at[4], one.at[3], (s + 1, b, h)).start()
            for k in range(2, B, 2):
                remote(hid_own, col_block(j_own), zs.at[k], zr.at[b], (s + 1, ahead(k), h)).start()

        for k in range(B):
            t = ahead(k)
            push(hid_own.at[pl.ds(pl.multiple_of(t * rows, rows), rows), :], hid_out.at[:, cols], hs.at[k], hr.at[j_own], t)
        for k in range(B):
            t = ahead(k)
            pushed(hid_own.at[pl.ds(0, rows), :], hs.at[k], t)
            pushed(cache_own.at[:, t], cs.at[k], t)

        @pl.when(s < S - 1)
        def _():
            remote(hid_own, col_block(j_own), one.at[4], one.at[3], (s + 1, b, h)).wait_send()
            for k in range(2, B, 2):
                remote(hid_own, col_block(j_own), zs.at[k], zr.at[b], (s + 1, ahead(k), h)).wait_send()

    for j in range(heads):
        cols = pl.ds(j * hd, hd)
        arrived(hid_out.at[:, cols], hr.at[j])
        arrived(cache_out.at[:, :, cols], cr.at[j])

    for k in range(heads):
        j = lax.rem(b + k, heads)
        pushed(w_in.at[:, :, cols_of(j)], ws.at[k], j + off)
        pushed(stale_in.at[:, :, cols_of(j)], ss.at[k], j + off)
    swap_cores().wait_send()

    @pl.when(s == 1)
    def _():
        for k in range(1, B):
            remote(G.at[b], G.at[b], gxs.at[k], gyr.at[b], (s - 1, b, h)).wait_send()
        for k in range(2, B, 2):
            remote(G.at[b], G.at[b], gzs.at[k], gzr.at[b], (s, ahead(k), h)).wait_send()
        for k in range(0, B, 2):
            remote(G.at[b], G.at[b], gys.at[k], gyr.at[b], (s, mate, h)).wait_send()

    @pl.when(s > 0)
    def _():
        block = col_block(0)

        for k in range(0, B, 2):
            c = ahead(k)

            @pl.when((c >= off) & (c < off + heads))
            def _():
                remote(block, block, ys.at[k], yr.at[b], (s, mate, h)).wait_send()


def shards(
    hidden_in, w_qkv, norm_gain, qk_gain, text_states, text_len, patch_len, stale_flags, stale_kv
):
    S, B = lax.axis_size("section"), lax.axis_size("blk")
    micro, tok, width = hidden_in.shape
    hd = qk_gain.shape[2]
    heads = width // hd
    rows = micro * tok
    total = B * rows
    depth = w_qkv.shape[1]
    text = text_states.shape[1]
    w = w_qkv[0].transpose(1, 0, 2)
    smem = pl.BlockSpec(memory_space=pltpu.SMEM)
    vmem = pl.BlockSpec(memory_space=pltpu.VMEM)
    hbm = pl.BlockSpec(memory_space=pl.ANY)
    sem = pltpu.SemaphoreType.DMA
    hid, cache = pl.pallas_call(
        functools.partial(kernel, (S, B, heads, hd, micro, tok)),
        out_shape=(
            jax.ShapeDtypeStruct((rows, width), BF16),
            jax.ShapeDtypeStruct((2, rows, width), BF16),
        ),
        in_specs=[smem] * 3 + [vmem, hbm, vmem, vmem, hbm, vmem],
        out_specs=(vmem, vmem),
        scratch_shapes=[
            pltpu.VMEM((B, rows, 2 * width), BF16),
            pltpu.VMEM((2, heads, total, hd), BF16),
            pltpu.VMEM((total, hd), BF16),
            pltpu.VMEM((B, rows, width), BF16),
            pltpu.VMEM((total, 2 * width), BF16),
            pltpu.VMEM((text, 2 * width), BF16),
            pltpu.VMEM((text, 2 * width), BF16),
            pltpu.VMEM((3, B * depth, hd), BF16),
            pltpu.VMEM((2, B, rows, hd), BF16),
            pltpu.VMEM((text, hd), BF16),
            pltpu.VMEM((text, hd), BF16),
            pltpu.VMEM((total, hd), BF16),
            pltpu.VMEM((2, B, rows, hd), BF16),
            sem((B,)), sem((B,)), sem((B,)), sem((B,)),
            sem((heads,)), sem((B,)), sem((heads,)), sem((B,)),
            sem((B,)), sem((heads,)), sem((B,)), sem((heads,)),
            sem((B,)), sem((B,)), sem((B,)), sem((B,)), sem((B + 1,)),
            sem((6,)),
        ],
        compiler_params=pltpu.CompilerParams(
            collective_id=0, has_side_effects=True, vmem_limit_bytes=60 * 1024 * 1024
        ),
    )(
        text_len, patch_len, stale_flags.T,
        hidden_in.reshape(rows, width), w, norm_gain, qk_gain[0], text_states[0],
        stale_kv[0].reshape(2, rows, width),
    )
    return (
        hid.reshape(1, micro, tok, width),
        cache.reshape(1, 2, micro, tok, width),
    )


def solution(mesh):
    in_specs = (
        P(None, "blk", "head"),
        P("section", "blk", None, "head"),
        P("section", None),
        P("section", None, None),
        P("section", None, None),
        P(),
        P(),
        P(),
        P("section", None, None, "blk", "head"),
    )
    out_specs = (P("section", None, "blk", "head"), P("section", None, None, "blk", "head"))
    return jax.shard_map(shards, mesh=mesh, in_specs=in_specs, out_specs=out_specs, check_vma=False)
```

profile of v0, /device:TPU:3, one launch (start us, length us, event | category | flops | bytes accessed | tf_op | source)
XLA Modules:
  0.0 57.0 jit_solution(3949425931462157211)
XLA Ops:
  1.3 53.6 %shard_map.104 = (bf16[32,768]{1,0:T(8,128)(2,1)}, bf16[2,32,768]{2,1,0:T(8,128)(2,1)}) custom-call(s32[1]{0:T(128)S(6)} %copy.13.text_len, s32[4]{0:T(128)} %patch_len.1, s32[2,4]{1,0:T(2,128)} %bitcast.16, bf16[32,768]{1,0:T(8,128)(2,1)} %bitcast.15, bf16[3,192,768]{2,1,0:T(8,128)(2,1)} %bitcast.10, f32[1,1536]{1,0:T(1,128)} %row_gain.1, ...), custom_call_target="tpu_custom_call" | custom-call | tf_op jit(solution)/shard_map/pallas_call | solution.py:324
  54.9 0.0 copy-start
  54.9 1.5 %copy.14 = bf16[1,4,8,768]{3,2,1,0:T(8,128)(2,1)} copy(bf16[1,4,8,768]{3,2,1,0:T(8,128)(2,1)} %bitcast.14) | data formatting | bytes 98304
  56.4 0.0 copy-done
  56.4 0.6 %copy.15 = bf16[1,2,4,8,768]{4,3,2,1,0:T(8,128)(2,1)} copy(bf16[1,2,4,8,768]{4,3,2,1,0:T(8,128)(2,1)S(1)} %bitcast.13) | data formatting | bytes 196608
Async XLA Ops:
  54.9 1.5 %copy-start = (bf16[2,32,768]{2,1,0:T(8,128)(2,1)S(1)}, bf16[2,32,768]{2,1,0:T(8,128)(2,1)}, u32[]{:S(2)}) copy-start(bf16[2,32,768]{2,1,0:T(8,128)(2,1)} %get-tuple-element.5) | copy-start | bytes 294916
where the time goes:
time: 57.3 us; the launch traced here: 57 us
  Pallas kernels  53.6 us (94%)
  local copies, waits for them, and re-layouts  2.1 us (4%)
  between operations  1.29 us (2%)
    pallas_call x1, Pallas kernels, shards(): pl.pallas_call(functools.partial(kernel, (S, B, heads, hd, micro, tok)),...  53.6 us
    unnamed x4, local copies, waits for them, and re-layouts  2.1 us

commit v1 on v0

v1 whole, which is shorter than its diff:
```python
import functools

import jax
import jax.numpy as jnp
from jax import lax
from jax.experimental import pallas as pl
from jax.experimental.pallas import tpu as pltpu
from jax.sharding import PartitionSpec as P

MESH = pl.DeviceIdType.MESH
F32 = jnp.float32
BF16 = jnp.bfloat16


def rms(values, gain):
    return values * lax.rsqrt(jnp.mean(values * values, axis=-1, keepdims=True) + 1e-06) * gain


def kernel(
    dims,
    text_len_in, patch_len_in, flags_in,
    hid_in, w_in, row_gain_in, head_gain_in, text_hbm, stale_in,
    hid_out, cache_out,
    text_len, patch_len, flags, row_gain, head_gain, ls,
    X, X1, RES, XN, text_in, TN, W, R, ST, TK, TV, hid_own, cache_own,
    all_in, clear, xs, xr, xfs, ws, wr, wrs, wcs, rr, fs, ss, sr,
    zs, zr, ys, yr, ms, mr, hs, hr, cs, cr, one,
):
    S, B, heads, hd, micro, tok = dims
    n = B // 2
    slots = (heads + 1) // 2
    rows = micro * tok
    total = B * rows
    width = heads * hd
    depth = w_in.shape[1]
    s, b, h = lax.axis_index("section"), lax.axis_index("blk"), lax.axis_index("head")
    first_owner = (B - heads) // 2
    off = first_owner - 1 + 2 * h if B - heads >= 2 else first_owner
    late = lax.rem(s, 2)
    pair = s + 1 - 2 * late
    mate = b + 1 - 2 * lax.rem(b, 2)
    my_half = b // n
    j_own = b - off
    owner = (b >= off) & (b < off + heads)
    half = pl.ds(pl.multiple_of(h * width, hd), width)
    other_half = pl.ds(pl.multiple_of((1 - h) * width, hd), width)

    def ahead(k):
        return lax.rem(b + k, B)

    def in_half(k):
        return my_half * n + lax.rem(b - my_half * n + k, n)

    def owns(c):
        return (c >= off) & (c < off + heads)

    def remote(src, dst, send, recv, dev):
        return pltpu.make_async_remote_copy(
            src_ref=src, dst_ref=dst, send_sem=send, recv_sem=recv, device_id=dev, device_id_type=MESH
        )

    def arrived(dst, sem):
        pltpu.make_async_copy(dst, dst, sem).wait()

    def sent(src, sem):
        remote(src, src, sem, sem, (s, b, 1 - h)).wait_send()

    def push(src, dst, send, recv, target):
        @pl.when(target == b)
        def _():
            pltpu.make_async_copy(src, dst, recv).start()

        @pl.when(target != b)
        def _():
            remote(src, dst, send, recv, (s, target, h)).start()

    def pushed(src, send, target):
        @pl.when(target != b)
        def _():
            sent(src, send)

    barrier = pltpu.get_barrier_semaphore()

    def hello(*dev):
        pl.semaphore_signal(barrier, inc=1, device_id=dev, device_id_type=MESH)

    across = lax.rem(b + n, B)
    for k in range(n):
        hello(pair, in_half(k), h)
    for k in range(1, n):
        hello(s, in_half(k), h)
    hello(s, b, 1 - h)
    hello(pair, across, h)
    hello(s, across, h)
    beside = jnp.where(late == 1, s + 1, s - 1)
    linked = (beside >= 0) & (beside < S)
    if S > 2:
        @pl.when(linked)
        def _():
            for k in range(0, B, 2):
                hello(beside, ahead(k), h)

    text_copy = pltpu.make_async_copy(text_hbm, text_in, one.at[5])
    text_copy.start()
    small = (
        (text_len_in, text_len), (patch_len_in, patch_len), (flags_in, flags),
        (row_gain_in, row_gain), (head_gain_in, head_gain),
    )
    loads = [pltpu.make_async_copy(src, dst, ls.at[i]) for i, (src, dst) in enumerate(small)]
    for load in loads:
        load.start()

    def row_block(c):
        return X.at[c, :, half]

    def col_block(j):
        return X1.at[h, j]

    @pl.when(s == 0)
    def _():
        pltpu.make_async_copy(hid_in, row_block(b), one.at[2]).start()

    with jax.named_scope("barrier"):
        pl.semaphore_wait(barrier, 2 * n + 2 + (linked.astype(jnp.int32) * n if S > 2 else 0))

    pl.semaphore_signal(all_in, inc=1, device_id=(s, across, h), device_id_type=MESH)

    @pl.when(s == 0)
    def _():
        remote(hid_in, row_block(b), xfs.at[0], xr.at[b], (s, mate, h)).start()

    def send_states(which):
        for k in range(2, B, 2):
            @pl.when((s == 1) & which(ahead(k)))
            def _():
                remote(hid_in, row_block(b), xs.at[k // 2], xr.at[b], (s - 1, ahead(k), h)).start()

    def cols_of(j):
        return pl.ds(pl.multiple_of(j * hd, hd), hd)

    def w_cols(j):
        return w_in.at[:, :, cols_of(j)]

    def w_rows(c):
        return W.at[:, pl.ds(pl.multiple_of(c * depth, depth), depth), :]

    def odd_head(c, t):
        return 2 * t + lax.rem(c + off + 1, 2)

    def even_head(c, t):
        return 2 * t + lax.rem(c + off, 2)

    def crosses(c, j):
        return (j < heads) & ((j + off) // n != c // n)

    def stays(j):
        return (j + off) // n == my_half

    def send_relayed():
        for t in range(slots):
            j = odd_head(b, t)

            @pl.when(crosses(b, j))
            def _():
                via = jnp.where(late == 1, b, mate)
                remote(w_cols(j), R.at[t], wrs.at[t], rr.at[t], (pair, via, h)).start()

    def near(c):
        return (c // n == my_half) | (c == across)

    def far(c):
        return jnp.logical_not(near(c))

    def send_crossing(which):
        for t in range(slots):
            j = even_head(b, t)

            @pl.when(crosses(b, j) & which(j + off))
            def _():
                remote(w_cols(j), w_rows(b), wcs.at[t], wr.at[b], (s, j + off, h)).start()

    def send_staying():
        for k in range(heads):
            j = lax.rem(b + k, heads)

            @pl.when(stays(j))
            def _():
                push(w_cols(j), w_rows(b), ws.at[k], wr.at[b], j + off)

    def send_stale(which):
        for k in range(heads):
            j = lax.rem(b + k, heads)

            @pl.when(which(j + off))
            def _():
                push(stale_in.at[:, :, cols_of(j)], ST.at[:, b], ss.at[k], sr.at[b], j + off)

    def sends_done():
        for t in range(slots):
            @pl.when(crosses(b, odd_head(b, t)))
            def _():
                sent(w_cols(0), wrs.at[t])

            @pl.when(crosses(b, even_head(b, t)))
            def _():
                sent(w_cols(0), wcs.at[t])

        for k in range(heads):
            j = lax.rem(b + k, heads)

            @pl.when(stays(j))
            def _():
                pushed(w_cols(j), ws.at[k], j + off)

            pushed(stale_in.at[:, :, cols_of(j)], ss.at[k], j + off)

    cb = jnp.where(late == 1, mate, b)

    def relayed(t):
        j = odd_head(cb, t)
        return crosses(cb, j), remote(R.at[t], w_rows(cb), fs.at[t], wr.at[cb], (pair, j + off, h))

    def relay():
        for t in range(slots):
            used, onward = relayed(t)

            @pl.when(used)
            def _():
                arrived(R.at[t], rr.at[t])
                onward.start()

    def relay_done():
        for t in range(slots):
            used, _ = relayed(t)

            @pl.when(used)
            def _():
                sent(R.at[t], fs.at[t])

    def all_clear():
        for k in range(2, n, 2):
            pl.semaphore_signal(clear, inc=1, device_id=(s, in_half(k), h), device_id_type=MESH)
        with jax.named_scope("clear"):
            pl.semaphore_wait(clear, n // 2 - 1)

    inner = lax.rem(b, n) // (n // 2) != my_half
    outer = jnp.logical_not(inner)
    early = late == 0

    send_states(near)

    @pl.when(early)
    def _():
        send_relayed()
        send_stale(near)

    @pl.when(inner)
    def _():
        send_crossing(near)

    @pl.when(early & outer)
    def _():
        send_staying()

    with jax.named_scope("all_in"):
        pl.semaphore_wait(all_in, 1)

    send_states(far)

    @pl.when(early)
    def _():
        @pl.when(inner)
        def _():
            send_crossing(far)

        @pl.when(outer)
        def _():
            send_crossing(near)
            send_crossing(far)

        send_stale(far)

        @pl.when(inner)
        def _():
            send_staying()

    @pl.when(s == 0)
    def _():
        with jax.named_scope("xcol"):
            for k in range(2, B, 2):
                c = ahead(k)
                arrived(row_block(c), xr.at[c])
                remote(row_block(c), row_block(c), xfs.at[k // 2], xr.at[c], (s, mate, h)).start()

    for load in loads:
        load.wait()
    text_copy.wait()

    @pl.when(owner)
    def _():
        TN[...] = rms(text_in[...].astype(F32), row_gain[...]).astype(BF16)

    @pl.when(late == 1)
    def _():
        with jax.named_scope("relay"):
            relay()
        with jax.named_scope("relay_done"):
            relay_done()
        send_relayed()
        all_clear()


        @pl.when(outer)
        def _():
            send_staying()
            send_crossing(near)

        send_crossing(far)

        @pl.when(inner)
        def _():
            send_staying()

        send_stale(near)
        send_stale(far)

    def norm_states(values):
        values = values.astype(F32)
        XN[...] = rms(values, row_gain[...]).astype(BF16)

    def swap_cores():
        return remote(X.at[:, :, half], X.at[:, :, half], one.at[0], one.at[1], (s, b, 1 - h))

    @pl.when(s == 0)
    def _():
        with jax.named_scope("waitX"):
            pltpu.make_async_copy(hid_in, row_block(b), one.at[2]).wait()
            for k in range(0, B, 2):
                c = lax.rem(mate + k, B)
                arrived(row_block(c), xr.at[c])

        swap_cores().start()
        with jax.named_scope("waitswap"):
            arrived(X.at[:, :, other_half], one.at[1])

        @pl.when(owner)
        def _():
            norm_states(X[...].reshape(total, 2 * width))
            RES[...] = X[:, :, pl.ds(pl.multiple_of(h * width + j_own * hd, hd), hd)].reshape(total, hd)

    @pl.when(early)
    def _():
        with jax.named_scope("relay"):
            relay()

    def to_core(c, k):
        return remote(col_block(c - off), col_block(c - off), ms.at[k], mr.at[c - off], (s, b, 1 - h))

    @pl.when(s > 0)
    def _():
        with jax.named_scope("waitX1"):
            for k in range(0, B, 2):
                c = ahead(k)

                @pl.when(owns(c))
                def _():
                    block = col_block(c - off)
                    arrived(block, zr.at[c])
                    remote(block, block, ys.at[k], yr.at[c], (s, mate, h)).start()
                    to_core(c, k).start()

        with jax.named_scope("waitX1m"):
            for k in range(0, B, 2):
                c = lax.rem(mate + k, B)

                @pl.when(owns(c))
                def _():
                    arrived(col_block(c - off), yr.at[c])
                    to_core(c, k + 1).start()

        with jax.named_scope("waitX1c"):
            for j in range(heads):
                arrived(X1.at[1 - h, j], mr.at[j])

        @pl.when(owner)
        def _():
            norm_states(
                jnp.concatenate([X1[i, j] for i in range(2) for j in range(heads)], axis=1)
            )
            RES[...] = X1[h, j_own]

    @pl.when(owner)
    def _():
        with jax.named_scope("waitW"):
            for c in range(B):
                arrived(W.at[:, pl.ds(c * depth, depth), :], wr.at[c])
        text_kv = jnp.dot(
            TN[...], jnp.concatenate([W[1], W[2]], axis=1), preferred_element_type=F32
        ).astype(BF16)
        TK[...] = rms(text_kv[:, :hd].astype(F32), head_gain[1:2, :]).astype(BF16)
        TV[...] = text_kv[:, hd:]
        proj = jnp.dot(
            XN[...], jnp.concatenate([W[0], W[1], W[2]], axis=1), preferred_element_type=F32
        )
        fresh_k = proj[:, hd : 2 * hd].astype(BF16)
        fresh_v = proj[:, 2 * hd :].astype(BF16)
        cache_own[0] = fresh_k.reshape(B, rows, hd)
        cache_own[1] = fresh_v.reshape(B, rows, hd)
        cols = cols_of(j_own)

        def push_cache():
            for k in range(B):
                t = ahead(k)
                push(cache_own.at[:, t], cache_out.at[:, :, cols], cs.at[k], cr.at[j_own], t)

        @pl.when(s == S - 1)
        def _():
            push_cache()

        with jax.named_scope("waitST"):
            for c in range(B):
                arrived(ST.at[:, c], sr.at[c])
        tok_bits = tok.bit_length() - 1

        def place(shape, axis):
            at = lax.broadcasted_iota(jnp.int32, shape, axis)
            which = lax.shift_right_logical(at, tok_bits) & (micro - 1)
            spot = lax.shift_right_logical(at, rows.bit_length() - 1) * tok + (at & (tok - 1))
            return which, spot

        def per_micro(which, read):
            out = jnp.zeros(which.shape, jnp.int32)
            for m in range(micro):
                out = jnp.where(which == m, read(m), out)
            return out

        which, _ = place((total, hd), 0)
        use_stale = per_micro(which, lambda m: flags[s, m]) == 1
        kept_k = jnp.where(use_stale, ST[0].reshape(total, hd).astype(F32), fresh_k.astype(F32))
        kept_v = jnp.where(use_stale, ST[1].reshape(total, hd).astype(F32), fresh_v.astype(F32))
        keys = rms(kept_k, head_gain[1:2, :]).astype(BF16)
        queries = rms(proj[:, :hd], head_gain[0:1, :]).astype(BF16)
        scale = hd**-0.5
        nt = (((1,), (1,)), ((), ()))

        def attend(key_rows, value_rows, mask):
            scores = lax.dot_general(queries, key_rows, nt, preferred_element_type=F32) * scale
            probs = jnp.where(mask, jnp.exp(scores), 0.0)
            num = jnp.dot(probs.astype(BF16), value_rows, preferred_element_type=F32)
            return num, jnp.sum(probs, axis=1, keepdims=True)

        shape = (total, total)
        q_which, _ = place(shape, 0)
        k_which, k_spot = place(shape, 1)
        mask = (q_which == k_which) & (k_spot < per_micro(k_which, lambda m: patch_len[m]))
        num, den = attend(keys, kept_v.astype(BF16), mask)
        text_at = lax.broadcasted_iota(jnp.int32, (total, TK.shape[0]), 1)
        text_num, text_den = attend(TK[...], TV[...], text_at < text_len[0])
        attended = (num + text_num) / (den + text_den)
        hid_own[...] = (RES[...].astype(F32) + attended).astype(BF16)

        @pl.when(s < S - 1)
        def _():
            for k in range(0, B, 2):
                remote(hid_own, col_block(j_own), zs.at[k], zr.at[b], (s + 1, ahead(k), h)).start()

        @pl.when(s < S - 1)
        def _():
            for k in range(0, B, 2):
                sent(hid_own, zs.at[k])

        for k in range(B):
            t = ahead(k)
            push(hid_own.at[pl.ds(pl.multiple_of(t * rows, rows), rows), :], hid_out.at[:, cols], hs.at[k], hr.at[j_own], t)
        @pl.when(s < S - 1)
        def _():
            push_cache()

    with jax.named_scope("waitOut"):
        for j in range(heads):
            cols = pl.ds(j * hd, hd)
            arrived(hid_out.at[:, cols], hr.at[j])
            arrived(cache_out.at[:, :, cols], cr.at[j])

    @pl.when(owner)
    def _():
        for k in range(B):
            t = ahead(k)
            pushed(hid_own.at[pl.ds(0, rows), :], hs.at[k], t)
            pushed(cache_own.at[:, t], cs.at[k], t)

    sends_done()

    @pl.when(late == 0)
    def _():
        relay_done()

    @pl.when(s == 0)
    def _():
        swap_cores().wait_send()
        for k in range(n):
            sent(hid_in, xfs.at[k])

    @pl.when(s == 1)
    def _():
        for k in range(1, n):
            sent(hid_in, xs.at[k])

    @pl.when(s > 0)
    def _():
        block = col_block(0)
        for k in range(0, B, 2):
            @pl.when(owns(ahead(k)))
            def _():
                sent(block, ys.at[k])
                sent(block, ms.at[k])

            @pl.when(owns(lax.rem(mate + k, B)))
            def _():
                sent(block, ms.at[k + 1])


def shards(
    hidden_in, w_qkv, norm_gain, qk_gain, text_states, text_len, patch_len, stale_flags, stale_kv
):
    S, B = lax.axis_size("section"), lax.axis_size("blk")
    micro, tok, width = hidden_in.shape
    hd = qk_gain.shape[2]
    heads = width // hd
    rows = micro * tok
    total = B * rows
    depth = w_qkv.shape[1]
    text = text_states.shape[1]
    n, slots = B // 2, (heads + 1) // 2
    w = w_qkv[0].transpose(1, 0, 2)
    vmem = pl.BlockSpec(memory_space=pltpu.VMEM)
    hbm = pl.BlockSpec(memory_space=pltpu.HBM)
    sem = pltpu.SemaphoreType.DMA
    hid, cache = pl.pallas_call(
        functools.partial(kernel, (S, B, heads, hd, micro, tok)),
        out_shape=(
            pltpu.VMEM((rows, width), BF16),
            pltpu.VMEM((2, rows, width), BF16),
        ),
        in_specs=[hbm] * 9,
        out_specs=(vmem, vmem),
        scratch_shapes=[
            pltpu.SMEM(text_len.shape, jnp.int32),
            pltpu.SMEM(patch_len.shape, jnp.int32),
            pltpu.SMEM(stale_flags.shape[::-1], jnp.int32),
            pltpu.VMEM(norm_gain.shape, F32),
            pltpu.VMEM(qk_gain.shape[1:], F32),
            sem((5,)),
            pltpu.VMEM((B, rows, 2 * width), BF16),
            pltpu.VMEM((2, heads, total, hd), BF16),
            pltpu.VMEM((total, hd), BF16),
            pltpu.VMEM((total, 2 * width), BF16),
            pltpu.VMEM((text, 2 * width), BF16),
            pltpu.VMEM((text, 2 * width), BF16),
            pltpu.VMEM((3, B * depth, hd), BF16),
            pltpu.VMEM((slots, 3, depth, hd), BF16),
            pltpu.VMEM((2, B, rows, hd), BF16),
            pltpu.VMEM((text, hd), BF16),
            pltpu.VMEM((text, hd), BF16),
            pltpu.VMEM((total, hd), BF16),
            pltpu.VMEM((2, B, rows, hd), BF16),
            pltpu.SemaphoreType.REGULAR, pltpu.SemaphoreType.REGULAR,
            sem((n,)), sem((B,)), sem((n,)),
            sem((heads,)), sem((B,)), sem((slots,)), sem((slots,)), sem((slots,)), sem((slots,)),
            sem((heads,)), sem((B,)),
            sem((B,)), sem((B,)), sem((B,)), sem((B,)), sem((B,)), sem((heads,)),
            sem((B,)), sem((heads,)), sem((B,)), sem((heads,)),
            sem((6,)),
        ],
        compiler_params=pltpu.CompilerParams(
            collective_id=0, has_side_effects=True, vmem_limit_bytes=60 * 1024 * 1024
        ),
    )(
        text_len, patch_len, stale_flags.T,
        hidden_in.reshape(rows, width), w, norm_gain, qk_gain[0], text_states[0],
        stale_kv[0].reshape(2, rows, width),
    )
    return (
        hid.reshape(1, micro, tok, width),
        cache.reshape(1, 2, micro, tok, width),
    )


def solution(mesh):
    in_specs = (
        P(None, "blk", "head"),
        P("section", "blk", None, "head"),
        P("section", None),
        P("section", None, None),
        P("section", None, None),
        P(),
        P(),
        P(),
        P("section", None, None, "blk", "head"),
    )
    out_specs = (P("section", None, "blk", "head"), P("section", None, None, "blk", "head"))
    return jax.shard_map(shards, mesh=mesh, in_specs=in_specs, out_specs=out_specs, check_vma=False)
```

time: 57.3 us -> 52.5 us (0.916)
  Pallas kernels: 53.6 us -> 49.8 us
  local copies, waits for them, and re-layouts: 2.1 us -> 1.26 us
    pallas_call x1, Pallas kernels: 53.6 us -> 49.8 us  [shards(): pl.pallas_call(functools.partial(kernel, (S, B, heads, hd, micro, tok)),...]
    unnamed x4 -> x2, local copies, waits for them, and re-layouts: 2.1 us -> 1.26 us
where the time goes in v1:
time: 52.5 us; the launch traced here: 52.3 us
  Pallas kernels  49.8 us (95%)
  between operations  1.29 us (2%)
  local copies, waits for them, and re-layouts  1.26 us (2%)
    pallas_call x1, Pallas kernels, shards(): pl.pallas_call(functools.partial(kernel, (S, B, heads, hd, micro, tok)),...  49.8 us
    unnamed x2, local copies, waits for them, and re-layouts  1.26 us

profile of v1, /device:TPU:3, one launch (start us, length us, event | category | flops | bytes accessed | tf_op | source)
XLA Modules:
  0.0 52.3 jit_solution(4858372117716852686)
XLA Ops:
  1.3 49.8 %shard_map.104 = (bf16[32,768]{1,0:T(8,128)(2,1)S(1)}, bf16[2,32,768]{2,1,0:T(8,128)(2,1)S(1)}) custom-call(s32[1]{0:T(128)S(6)} %copy.15.text_len_in, s32[4]{0:T(128)} %patch_len_in.1, s32[2,4]{1,0:T(2,128)} %bitcast.16, bf16[32,768]{1,0:T(8,128)(2,1)} %bitcast.15, bf16[3,192,768]{2,1,0:T(8,128)(2,1)} %bitcast.12, f32[1,1536]{1,0:T(1,128)} %row_gain_in.1, ...), custom_call_target="tpu_custom_call" | custom-call | tf_op jit(solution)/shard_map/pallas_call | solution.py:539
  51.1 0.6 %copy.13 = bf16[1,4,8,768]{3,2,1,0:T(8,128)(2,1)} copy(bf16[1,4,8,768]{3,2,1,0:T(8,128)(2,1)S(1)} %bitcast.11) | data formatting | bytes 98304
  51.7 0.6 %copy.14 = bf16[1,2,4,8,768]{4,3,2,1,0:T(8,128)(2,1)} copy(bf16[1,2,4,8,768]{4,3,2,1,0:T(8,128)(2,1)S(1)} %bitcast.10) | data formatting | bytes 196608

commit v2 on v1

v2 whole, which is shorter than its diff:
```python
import functools

import jax
import jax.numpy as jnp
from jax import lax
from jax.experimental import pallas as pl
from jax.experimental.pallas import tpu as pltpu
from jax.sharding import PartitionSpec as P

MESH = pl.DeviceIdType.MESH
F32 = jnp.float32
BF16 = jnp.bfloat16


def rms(values, gain):
    return values * lax.rsqrt(jnp.mean(values * values, axis=-1, keepdims=True) + 1e-06) * gain


def kernel(
    dims,
    text_len_in, patch_len_in, flags_in,
    hid_in, w_in, row_gain_in, head_gain_in, text_hbm, stale_in,
    hid_out, cache_out,
    text_len, patch_len, flags, row_gain, head_gain,
    X, X1, RES, XN, text_in, TN, W, R, PROJ, TKV, ST, TK, TV,
    hid_own, cache_own,
    all_in, clear, ls, xr, zs, zr, yr, rr, fs, one,
):
    S, B, heads, hd, micro, tok = dims
    n = B // 2
    slots = (heads + 1) // 2
    rows = micro * tok
    total = B * rows
    width = heads * hd
    depth = w_in.shape[1]
    s, b, h = lax.axis_index("section"), lax.axis_index("blk"), lax.axis_index("head")
    first_owner = (B - heads) // 2
    off = first_owner - 1 + 2 * h if B - heads >= 2 else first_owner
    late = lax.rem(s, 2)
    early = late == 0
    pair = s + 1 - 2 * late
    mate = b + 1 - 2 * lax.rem(b, 2)
    my_half = b // n
    across = lax.rem(b + n, B)
    inner = lax.rem(b, n) // (n // 2) != my_half
    outer = jnp.logical_not(inner)
    j_own = b - off
    owner = (b >= off) & (b < off + heads)
    core = (s, b, 1 - h)
    half = pl.ds(pl.multiple_of(h * width, hd), width)
    other_half = pl.ds(pl.multiple_of((1 - h) * width, hd), width)
    (
        w_send, w_recv, st_send, st_recv, x_send, xm_send, xc_send, xc_recv, x_own, text_recv,
        ym_send, core_send, core_recv, hid_send, hid_recv, cache_send, cache_recv,
    ) = [one.at[i] for i in range(17)]

    def ahead(k):
        return lax.rem(b + k, B)

    def in_half(k):
        return my_half * n + lax.rem(b - my_half * n + k, n)

    def nearest(k):
        return in_half(k) if k < n else lax.rem(in_half(k - n) + n, B)

    def owns(c):
        return (c >= off) & (c < off + heads)

    def near(c):
        return (c // n == my_half) | (c == across)

    def far(c):
        return jnp.logical_not(near(c))

    def remote(src, dst, send, recv, dev):
        return pltpu.make_async_remote_copy(
            src_ref=src, dst_ref=dst, send_sem=send, recv_sem=recv, device_id=dev, device_id_type=MESH
        )

    def arrived(dst, sem):
        pltpu.make_async_copy(dst, dst, sem).wait()

    def sent(src, sem):
        remote(src, src, sem, sem, core).wait_send()

    def push(src, dst, send, recv, target):
        @pl.when(target == b)
        def _():
            pltpu.make_async_copy(src, dst, recv).start()

        @pl.when(target != b)
        def _():
            remote(src, dst, send, recv, (s, target, h)).start()

    def cols_of(j):
        return pl.ds(pl.multiple_of(j * hd, hd), hd)

    def w_cols(j):
        return w_in.at[:, :, cols_of(j)]

    def w_rows(c):
        return W.at[:, pl.ds(pl.multiple_of(c * depth, depth), depth), :]

    def row_block(c):
        return X.at[c, :, half]

    barrier = pltpu.get_barrier_semaphore()

    def hello(*dev):
        pl.semaphore_signal(barrier, inc=1, device_id=dev, device_id_type=MESH)

    for k in range(n):
        hello(pair, in_half(k), h)
    for k in range(1, n):
        hello(s, in_half(k), h)
    hello(*core)
    hello(pair, across, h)
    hello(s, across, h)
    beside = jnp.where(late == 1, s + 1, s - 1)
    linked = (beside >= 0) & (beside < S)
    if S > 2:
        @pl.when(linked)
        def _():
            for k in range(0, B, 2):
                hello(beside, ahead(k), h)

    text_copy = pltpu.make_async_copy(text_hbm, text_in, text_recv)
    text_copy.start()
    small = (
        (text_len_in, text_len), (patch_len_in, patch_len), (flags_in, flags),
        (row_gain_in, row_gain), (head_gain_in, head_gain),
    )
    loads = [pltpu.make_async_copy(src, dst, ls.at[i]) for i, (src, dst) in enumerate(small)]
    for load in loads:
        load.start()

    @pl.when(s == 0)
    def _():
        pltpu.make_async_copy(hid_in, row_block(b), x_own).start()

    for load in loads:
        load.wait()
    text_copy.wait()
    TN[...] = rms(text_in[...].astype(F32), row_gain[...]).astype(BF16)

    with jax.named_scope("barrier"):
        pl.semaphore_wait(barrier, 2 * n + 2 + (linked.astype(jnp.int32) * n if S > 2 else 0))

    pl.semaphore_signal(all_in, inc=1, device_id=(s, across, h), device_id_type=MESH)

    def other_side(c, t):
        return 2 * t + lax.rem(c + off + 1, 2)

    def same_side(c, t):
        return 2 * t + lax.rem(c + off, 2)

    def crosses(c, j):
        return (j < heads) & ((j + off) // n != c // n)

    def send_relayed():
        for t in range(slots):
            j = other_side(b, t)

            @pl.when(crosses(b, j))
            def _():
                via = jnp.where(late == 1, b, mate)
                remote(w_cols(j), R.at[t], w_send, rr.at[t], (pair, via, h)).start()

    def send_crossing(which):
        for t in range(slots):
            j = same_side(b, t)

            @pl.when(crosses(b, j) & which(j + off))
            def _():
                remote(w_cols(j), w_rows(b), w_send, w_recv, (s, j + off, h)).start()

    def send_staying():
        for k in range(heads):
            j = lax.rem(b + k, heads)

            @pl.when((j + off) // n == my_half)
            def _():
                push(w_cols(j), w_rows(b), w_send, w_recv, j + off)

    def send_stale(which):
        for k in range(heads):
            j = lax.rem(b + k, heads)

            @pl.when(which(j + off))
            def _():
                push(stale_in.at[:, :, cols_of(j)], ST.at[:, b], st_send, st_recv, j + off)

    cb = jnp.where(late == 1, mate, b)

    def relayed(t):
        j = other_side(cb, t)
        return crosses(cb, j), remote(R.at[t], w_rows(cb), fs.at[t], w_recv, (pair, j + off, h))

    def relay():
        for t in range(slots):
            used, onward = relayed(t)

            @pl.when(used)
            def _():
                arrived(R.at[t], rr.at[t])
                onward.start()

    def relay_done():
        for t in range(slots):
            used, _ = relayed(t)

            @pl.when(used)
            def _():
                sent(R.at[t], fs.at[t])

    def send_states(which):
        for k in range(2, B, 2):
            @pl.when(which(nearest(k)))
            def _():
                remote(hid_in, row_block(b), x_send, xr.at[b], (s - 1, nearest(k), h)).start()

    def block_to_core(c):
        return remote(row_block(c), row_block(c), xc_send, xc_recv, core)

    @pl.when(s == 1)
    def _():
        send_states(near)

    @pl.when(early)
    def _():
        send_relayed()

        @pl.when(s == 0)
        def _():
            pltpu.make_async_copy(hid_in, row_block(b), x_own).wait()
            remote(row_block(b), row_block(b), xm_send, xr.at[b], (s, mate, h)).start()
            block_to_core(b).start()

        send_stale(near)

        @pl.when(inner)
        def _():
            send_crossing(near)

    with jax.named_scope("all_in"):
        pl.semaphore_wait(all_in, 1)

    @pl.when(early)
    def _():
        send_stale(far)

        @pl.when(outer)
        def _():
            send_crossing(near)

        send_crossing(far)

        @pl.when(s == 0)
        def _():
            with jax.named_scope("xcol"):
                for k in range(2, B, 2):
                    c = nearest(k)
                    arrived(row_block(c), xr.at[c])
                    remote(row_block(c), row_block(c), xm_send, xr.at[c], (s, mate, h)).start()
                    block_to_core(c).start()

        send_staying()

    @pl.when(late == 1)
    def _():
        @pl.when(s == 1)
        def _():
            send_states(far)

        send_relayed()
        with jax.named_scope("relay"):
            relay()
        with jax.named_scope("relay_done"):
            relay_done()
        for k in range(2, n, 2):
            pl.semaphore_signal(clear, inc=1, device_id=(s, in_half(k), h), device_id_type=MESH)
        send_staying()
        with jax.named_scope("clear"):
            pl.semaphore_wait(clear, n // 2 - 1)
        send_crossing(near)
        send_crossing(far)
        send_stale(near)
        send_stale(far)

    def norm_states(values):
        XN[...] = rms(values.astype(F32), row_gain[...]).astype(BF16)

    @pl.when(s == 0)
    def _():
        with jax.named_scope("waitX"):
            for k in range(0, B, 2):
                c = nearest(k) + mate - b
                arrived(row_block(c), xr.at[c])
                block_to_core(c).start()
        with jax.named_scope("waitswap"):
            arrived(X.at[:, :, other_half], xc_recv)

        @pl.when(owner)
        def _():
            norm_states(X[...].reshape(total, 2 * width))
            RES[...] = X[:, :, pl.ds(pl.multiple_of(h * width + j_own * hd, hd), hd)]

    @pl.when(early & jnp.logical_not(owner))
    def _():
        with jax.named_scope("relayW1"):
            relay()

    def col_block(j):
        return X1.at[h, j]

    def to_core(c):
        return remote(col_block(c - off), col_block(c - off), core_send, core_recv, core)

    @pl.when(s > 0)
    def _():
        with jax.named_scope("waitX1"):
            for k in range(0, B, 2):
                c = nearest(k)

                @pl.when(owns(c))
                def _():
                    block = col_block(c - off)
                    arrived(block, zr.at[c - off])
                    remote(block, block, ym_send, yr.at[c - off], (s, mate, h)).start()
                    to_core(c).start()

        with jax.named_scope("waitX1m"):
            for k in range(0, B, 2):
                c = nearest(k) + mate - b

                @pl.when(owns(c))
                def _():
                    arrived(col_block(c - off), yr.at[c - off])
                    to_core(c).start()

        with jax.named_scope("waitX1c"):
            arrived(X1.at[1 - h], core_recv)

        @pl.when(owner)
        def _():
            norm_states(jnp.concatenate([X1[i, j] for i in range(2) for j in range(heads)], axis=1))
            RES[...] = X1[h, j_own].reshape(RES.shape)

    @pl.when(owner)
    def _():
        with jax.named_scope("waitW"):
            arrived(W, w_recv)
        w_kv = jnp.concatenate([W[1], W[2]], axis=1)
        TKV[...] = jnp.dot(TN[...], w_kv, preferred_element_type=F32).astype(BF16)
        PROJ[...] = jnp.dot(
            XN[...], jnp.concatenate([W[0], w_kv], axis=1), preferred_element_type=F32
        )

    @pl.when(owner)
    def _():
        fresh_k = PROJ[:, hd : 2 * hd].astype(BF16)
        fresh_v = PROJ[:, 2 * hd :].astype(BF16)
        cache_own[0] = fresh_k.reshape(B, rows, hd)
        cache_own[1] = fresh_v.reshape(B, rows, hd)
        cols = cols_of(j_own)

        def push_cache():
            for k in range(B):
                t = ahead(k)
                push(cache_own.at[:, t], cache_out.at[:, :, cols], cache_send, cache_recv, t)

        @pl.when(s == S - 1)
        def _():
            push_cache()

        TK[...] = rms(TKV[:, :hd].astype(F32), head_gain[1:2, :]).astype(BF16)
        TV[...] = TKV[:, hd:]
        with jax.named_scope("waitST"):
            arrived(ST, st_recv)
        tok_bits = tok.bit_length() - 1

        def place(shape, axis):
            at = lax.broadcasted_iota(jnp.int32, shape, axis)
            which = lax.shift_right_logical(at, tok_bits) & (micro - 1)
            spot = lax.shift_right_logical(at, rows.bit_length() - 1) * tok + (at & (tok - 1))
            return which, spot

        def per_micro(which, read):
            out = jnp.zeros(which.shape, jnp.int32)
            for m in range(micro):
                out = jnp.where(which == m, read(m), out)
            return out

        which, _ = place((total, hd), 0)
        use_stale = per_micro(which, lambda m: flags[s, m]) == 1
        kept_k = jnp.where(use_stale, ST[0].reshape(total, hd).astype(F32), fresh_k.astype(F32))
        kept_v = jnp.where(use_stale, ST[1].reshape(total, hd).astype(F32), fresh_v.astype(F32))
        keys = rms(kept_k, head_gain[1:2, :]).astype(BF16)
        queries = rms(PROJ[:, :hd], head_gain[0:1, :]).astype(BF16)
        scale = hd**-0.5
        nt = (((1,), (1,)), ((), ()))

        def attend(key_rows, value_rows, mask):
            scores = lax.dot_general(queries, key_rows, nt, preferred_element_type=F32) * scale
            probs = jnp.where(mask, jnp.exp(scores), 0.0)
            num = jnp.dot(probs.astype(BF16), value_rows, preferred_element_type=F32)
            return num, jnp.sum(probs, axis=1, keepdims=True)

        shape = (total, total)
        q_which, _ = place(shape, 0)
        k_which, k_spot = place(shape, 1)
        mask = (q_which == k_which) & (k_spot < per_micro(k_which, lambda m: patch_len[m]))
        num, den = attend(keys, kept_v.astype(BF16), mask)
        text_at = lax.broadcasted_iota(jnp.int32, (total, TK.shape[0]), 1)
        text_num, text_den = attend(TK[...], TV[...], text_at < text_len[0])
        attended = (num + text_num) / (den + text_den)
        hid_own[...] = (RES[...].reshape(total, hd).astype(F32) + attended).astype(BF16)

        @pl.when(s < S - 1)
        def _():
            for k in range(0, B, 2):
                remote(hid_own, col_block(j_own), zs.at[k // 2], zr.at[j_own], (s + 1, ahead(k), h)).start()

        @pl.when(early)
        def _():
            relay()

        @pl.when(s < S - 1)
        def _():
            for k in range(0, B, 2):
                sent(hid_own, zs.at[k // 2])

        for k in range(B):
            t = ahead(k)
            push(hid_own.at[pl.ds(pl.multiple_of(t * rows, rows), rows), :], hid_out.at[:, cols], hid_send, hid_recv, t)
        @pl.when(s < S - 1)
        def _():
            push_cache()

    with jax.named_scope("waitOut"):
        arrived(hid_out, hid_recv)
        arrived(cache_out, cache_recv)

    @pl.when(owner)
    def _():
        sent(hid_own.at[pl.ds(0, total - rows), :], hid_send)
        sent(cache_own.at[:, pl.ds(0, B - 1)], cache_send)
        sent(w_in.at[:, :, pl.ds(0, width - hd)], w_send)
        sent(stale_in.at[:, :, pl.ds(0, width - hd)], st_send)

    @pl.when(jnp.logical_not(owner))
    def _():
        sent(w_in, w_send)
        sent(stale_in, st_send)

    @pl.when(early)
    def _():
        relay_done()

    @pl.when(s == 0)
    def _():
        sent(X.at[pl.ds(0, n), :, half], xm_send)
        sent(X.at[:, :, half], xc_send)

    @pl.when(s == 1)
    def _():
        sent(X.at[pl.ds(0, n - 1), :, half], x_send)

    @pl.when(s > 0)
    def _():
        sent(X1.at[h, pl.ds(0, heads // 2)], ym_send)
        sent(X1.at[h], core_send)


def shards(
    hidden_in, w_qkv, norm_gain, qk_gain, text_states, text_len, patch_len, stale_flags, stale_kv
):
    S, B = lax.axis_size("section"), lax.axis_size("blk")
    micro, tok, width = hidden_in.shape
    hd = qk_gain.shape[2]
    heads = width // hd
    rows = micro * tok
    total = B * rows
    depth = w_qkv.shape[1]
    text = text_states.shape[1]
    n, slots = B // 2, (heads + 1) // 2
    w = w_qkv[0].transpose(1, 0, 2)
    hbm = pl.BlockSpec(memory_space=pltpu.HBM)
    sem = pltpu.SemaphoreType.DMA
    hid, cache = pl.pallas_call(
        functools.partial(kernel, (S, B, heads, hd, micro, tok)),
        out_shape=(
            pltpu.VMEM((rows, width), BF16),
            pltpu.VMEM((2, rows, width), BF16),
        ),
        in_specs=[hbm] * 9,
        out_specs=(pl.BlockSpec(memory_space=pl.ANY),) * 2,
        scratch_shapes=[
            pltpu.SMEM(text_len.shape, jnp.int32),
            pltpu.SMEM(patch_len.shape, jnp.int32),
            pltpu.SMEM(stale_flags.shape[::-1], jnp.int32),
            pltpu.VMEM(norm_gain.shape, F32),
            pltpu.VMEM(qk_gain.shape[1:], F32),
            pltpu.VMEM((B, rows, 2 * width), BF16),
            pltpu.VMEM((2, heads, total, hd), BF16),
            pltpu.VMEM((B, rows, hd), BF16),
            pltpu.VMEM((total, 2 * width), BF16),
            pltpu.VMEM((text, 2 * width), BF16),
            pltpu.VMEM((text, 2 * width), BF16),
            pltpu.VMEM((3, B * depth, hd), BF16),
            pltpu.VMEM((slots, 3, depth, hd), BF16),
            pltpu.VMEM((total, 3 * hd), F32),
            pltpu.VMEM((text, 2 * hd), BF16),
            pltpu.VMEM((2, B, rows, hd), BF16),
            pltpu.VMEM((text, hd), BF16),
            pltpu.VMEM((text, hd), BF16),
            pltpu.VMEM((total, hd), BF16),
            pltpu.VMEM((2, B, rows, hd), BF16),
            pltpu.SemaphoreType.REGULAR, pltpu.SemaphoreType.REGULAR,
            sem((5,)), sem((B,)), sem((n,)), sem((heads,)), sem((heads,)),
            sem((slots,)), sem((slots,)), sem((17,)),
        ],
        compiler_params=pltpu.CompilerParams(
            collective_id=0, has_side_effects=True, vmem_limit_bytes=60 * 1024 * 1024
        ),
    )(
        text_len, patch_len, stale_flags.T,
        hidden_in.reshape(rows, width), w, norm_gain, qk_gain[0], text_states[0],
        stale_kv[0].reshape(2, rows, width),
    )
    return (
        hid.reshape(1, micro, tok, width),
        cache.reshape(1, 2, micro, tok, width),
    )


def solution(mesh):
    in_specs = (
        P(None, "blk", "head"),
        P("section", "blk", None, "head"),
        P("section", None),
        P("section", None, None),
        P("section", None, None),
        P(),
        P(),
        P(),
        P("section", None, None, "blk", "head"),
    )
    out_specs = (P("section", None, "blk", "head"), P("section", None, None, "blk", "head"))
    return jax.shard_map(shards, mesh=mesh, in_specs=in_specs, out_specs=out_specs, check_vma=False)
```

time: 52.5 us -> 46.7 us (0.89)
  Pallas kernels: 49.8 us -> 44 us
    pallas_call x1, Pallas kernels: 49.8 us -> 44 us  [shards(): pl.pallas_call(functools.partial(kernel, (S, B, heads, hd, micro, tok)),...]
where the time goes in v2:
time: 46.7 us; the launch traced here: 46.6 us
  Pallas kernels  44 us (94%)
  between operations  1.29 us (3%)
  local copies, waits for them, and re-layouts  1.26 us (3%)
    pallas_call x1, Pallas kernels, shards(): pl.pallas_call(functools.partial(kernel, (S, B, heads, hd, micro, tok)),...  44 us
    unnamed x2, local copies, waits for them, and re-layouts  1.26 us

profile of v2, /device:TPU:3, one launch (start us, length us, event | category | flops | bytes accessed | tf_op | source)
XLA Modules:
  0.0 46.6 jit_solution(14366772061286217675)
XLA Ops:
  1.3 44.0 %shard_map.104 = (bf16[32,768]{1,0:T(8,128)(2,1)S(1)}, bf16[2,32,768]{2,1,0:T(8,128)(2,1)S(1)}) custom-call(s32[1]{0:T(128)S(6)} %copy.15.text_len_in, s32[4]{0:T(128)} %patch_len_in.1, s32[2,4]{1,0:T(2,128)} %bitcast.16, bf16[32,768]{1,0:T(8,128)(2,1)} %bitcast.15, bf16[3,192,768]{2,1,0:T(8,128)(2,1)} %bitcast.12, f32[1,1536]{1,0:T(1,128)} %row_gain_in.1, ...), custom_call_target="tpu_custom_call" | custom-call | tf_op jit(solution)/shard_map/pallas_call | solution.py:490
  45.3 0.6 %copy.13 = bf16[1,4,8,768]{3,2,1,0:T(8,128)(2,1)} copy(bf16[1,4,8,768]{3,2,1,0:T(8,128)(2,1)S(1)} %bitcast.11) | data formatting | bytes 98304
  45.9 0.6 %copy.14 = bf16[1,2,4,8,768]{4,3,2,1,0:T(8,128)(2,1)} copy(bf16[1,2,4,8,768]{4,3,2,1,0:T(8,128)(2,1)S(1)} %bitcast.10) | data formatting | bytes 196608

commit v3 on v2

--- a/solution.py
+++ b/solution.py
@@ -22,9 +22,9 @@
     hid_in, w_in, row_gain_in, head_gain_in, text_hbm, stale_in,
     hid_out, cache_out,
     text_len, patch_len, flags, row_gain, head_gain,
-    X, X1, RES, XN, text_in, TN, W, R, PROJ, TKV, ST, TK, TV,
+    X, X1, RES, XN, text_in, TN, W, R, PROJ, ST, TK, TV,
     hid_own, cache_own,
-    all_in, clear, ls, xr, zs, zr, yr, rr, fs, one,
+    all_in, clear, taken, ls, xr, zs, zr, yr, rr, fs, one,
 ):
     S, B, heads, hd, micro, tok = dims
     n = B // 2
@@ -61,7 +61,7 @@
         return my_half * n + lax.rem(b - my_half * n + k, n)
 
     def nearest(k):
-        return in_half(k) if k < n else lax.rem(in_half(k - n) + n, B)
+        return in_half(k) if k < n else k + my_half * (2 * n - 2 - 2 * k) + lax.rem(b, 2)
 
     def owns(c):
         return (c >= off) & (c < off + heads)
@@ -151,26 +151,28 @@
     def other_side(c, t):
         return 2 * t + lax.rem(c + off + 1, 2)
 
-    def same_side(c, t):
-        return 2 * t + lax.rem(c + off, 2)
+    def central(c):
+        return lax.rem(c, n) // (n // 2) != c // n
 
     def crosses(c, j):
         return (j < heads) & ((j + off) // n != c // n)
+
+    def detours(c, j):
+        return crosses(c, j) & (lax.rem(j + off + c, 2) == 1)
 
     def send_relayed():
         for t in range(slots):
             j = other_side(b, t)
 
-            @pl.when(crosses(b, j))
-            def _():
-                via = jnp.where(late == 1, b, mate)
-                remote(w_cols(j), R.at[t], w_send, rr.at[t], (pair, via, h)).start()
+            @pl.when(detours(b, j))
+            def _():
+                remote(w_cols(j), R.at[t], w_send, rr.at[t], (pair, jnp.where(late == 1, b, mate), h)).start()
 
     def send_crossing(which):
-        for t in range(slots):
-            j = same_side(b, t)
-
-            @pl.when(crosses(b, j) & which(j + off))
+        for k in range(heads):
+            j = lax.rem(b + k, heads)
+
+            @pl.when(crosses(b, j) & jnp.logical_not(detours(b, j)) & which(j + off))
             def _():
                 remote(w_cols(j), w_rows(b), w_send, w_recv, (s, j + off, h)).start()
 
@@ -190,11 +192,10 @@
             def _():
                 push(stale_in.at[:, :, cols_of(j)], ST.at[:, b], st_send, st_recv, j + off)
 
-    cb = jnp.where(late == 1, mate, b)
-
     def relayed(t):
+        cb = jnp.where(late == 1, mate, b)
         j = other_side(cb, t)
-        return crosses(cb, j), remote(R.at[t], w_rows(cb), fs.at[t], w_recv, (pair, j + off, h))
+        return detours(cb, j), remote(R.at[t], w_rows(cb), fs.at[t], w_recv, (pair, j + off, h))
 
     def relay():
         for t in range(slots):
@@ -275,11 +276,11 @@
         send_relayed()
         with jax.named_scope("relay"):
             relay()
+        send_staying()
         with jax.named_scope("relay_done"):
             relay_done()
         for k in range(2, n, 2):
             pl.semaphore_signal(clear, inc=1, device_id=(s, in_half(k), h), device_id_type=MESH)
-        send_staying()
         with jax.named_scope("clear"):
             pl.semaphore_wait(clear, n // 2 - 1)
         send_crossing(near)
@@ -310,6 +311,21 @@
         with jax.named_scope("relayW1"):
             relay()
 
+    def text_part():
+        @pl.when(owner)
+        def _():
+            with jax.named_scope("waitW"):
+                arrived(W, w_recv)
+            text_kv = jnp.dot(
+                TN[...], jnp.concatenate([W[1], W[2]], axis=1), preferred_element_type=F32
+            ).astype(BF16)
+            TK[...] = rms(text_kv[:, :hd].astype(F32), head_gain[1:2, :]).astype(BF16)
+            TV[...] = text_kv[:, hd:]
+
+    @pl.when(s == 0)
+    def _():
+        text_part()
+
     def col_block(j):
         return X1.at[h, j]
 
@@ -329,6 +345,7 @@
                     remote(block, block, ym_send, yr.at[c - off], (s, mate, h)).start()
                     to_core(c).start()
 
+        pl.semaphore_signal(taken, inc=1, device_id=(s - 1, b, h), device_id_type=MESH)
         with jax.named_scope("waitX1m"):
             for k in range(0, B, 2):
                 c = nearest(k) + mate - b
@@ -338,6 +355,7 @@
                     arrived(col_block(c - off), yr.at[c - off])
                     to_core(c).start()
 
+        text_part()
         with jax.named_scope("waitX1c"):
             arrived(X1.at[1 - h], core_recv)
 
@@ -348,13 +366,22 @@
 
     @pl.when(owner)
     def _():
-        with jax.named_scope("waitW"):
-            arrived(W, w_recv)
-        w_kv = jnp.concatenate([W[1], W[2]], axis=1)
-        TKV[...] = jnp.dot(TN[...], w_kv, preferred_element_type=F32).astype(BF16)
         PROJ[...] = jnp.dot(
-            XN[...], jnp.concatenate([W[0], w_kv], axis=1), preferred_element_type=F32
+            XN[...], jnp.concatenate([W[0], W[1], W[2]], axis=1), preferred_element_type=F32
         )
+
+    def push_cache():
+        for k in range(B):
+            t = ahead(k)
+            push(cache_own.at[:, t], cache_out.at[:, :, cols_of(j_own)], cache_send, cache_recv, t)
+
+    def push_hidden():
+        for k in range(B):
+            t = ahead(k)
+            push(
+                hid_own.at[pl.ds(pl.multiple_of(t * rows, rows), rows), :],
+                hid_out.at[:, cols_of(j_own)], hid_send, hid_recv, t,
+            )
 
     @pl.when(owner)
     def _():
@@ -362,19 +389,10 @@
         fresh_v = PROJ[:, 2 * hd :].astype(BF16)
         cache_own[0] = fresh_k.reshape(B, rows, hd)
         cache_own[1] = fresh_v.reshape(B, rows, hd)
-        cols = cols_of(j_own)
-
-        def push_cache():
-            for k in range(B):
-                t = ahead(k)
-                push(cache_own.at[:, t], cache_out.at[:, :, cols], cache_send, cache_recv, t)
-
         @pl.when(s == S - 1)
         def _():
             push_cache()
 
-        TK[...] = rms(TKV[:, :hd].astype(F32), head_gain[1:2, :]).astype(BF16)
-        TV[...] = TKV[:, hd:]
         with jax.named_scope("waitST"):
             arrived(ST, st_recv)
         tok_bits = tok.bit_length() - 1
@@ -425,16 +443,20 @@
         def _():
             relay()
 
-        @pl.when(s < S - 1)
+        @pl.when(s == S - 1)
+        def _():
+            push_hidden()
+
+    @pl.when(s < S - 1)
+    def _():
+        with jax.named_scope("taken"):
+            pl.semaphore_wait(taken, 1)
+
+        @pl.when(owner)
         def _():
             for k in range(0, B, 2):
                 sent(hid_own, zs.at[k // 2])
-
-        for k in range(B):
-            t = ahead(k)
-            push(hid_own.at[pl.ds(pl.multiple_of(t * rows, rows), rows), :], hid_out.at[:, cols], hid_send, hid_recv, t)
-        @pl.when(s < S - 1)
-        def _():
+            push_hidden()
             push_cache()
 
     with jax.named_scope("waitOut"):
@@ -470,6 +492,17 @@
     def _():
         sent(X1.at[h, pl.ds(0, heads // 2)], ym_send)
         sent(X1.at[h], core_send)
+
+
+def store(hid, cache, hid_out, cache_out, done):
+    copies = (
+        pltpu.make_async_copy(hid, hid_out, done.at[0]),
+        pltpu.make_async_copy(cache, cache_out, done.at[1]),
+    )
+    for copy in copies:
+        copy.start()
+    for copy in copies:
+        copy.wait()
 
 
 def shards(
@@ -510,13 +543,12 @@
             pltpu.VMEM((3, B * depth, hd), BF16),
             pltpu.VMEM((slots, 3, depth, hd), BF16),
             pltpu.VMEM((total, 3 * hd), F32),
-            pltpu.VMEM((text, 2 * hd), BF16),
             pltpu.VMEM((2, B, rows, hd), BF16),
             pltpu.VMEM((text, hd), BF16),
             pltpu.VMEM((text, hd), BF16),
             pltpu.VMEM((total, hd), BF16),
             pltpu.VMEM((2, B, rows, hd), BF16),
-            pltpu.SemaphoreType.REGULAR, pltpu.SemaphoreType.REGULAR,
+            pltpu.SemaphoreType.REGULAR, pltpu.SemaphoreType.REGULAR, pltpu.SemaphoreType.REGULAR,
             sem((5,)), sem((B,)), sem((n,)), sem((heads,)), sem((heads,)),
             sem((slots,)), sem((slots,)), sem((17,)),
         ],
@@ -528,6 +560,16 @@
         hidden_in.reshape(rows, width), w, norm_gain, qk_gain[0], text_states[0],
         stale_kv[0].reshape(2, rows, width),
     )
+    hid, cache = pl.pallas_call(
+        store,
+        out_shape=(
+            jax.ShapeDtypeStruct(hid.shape, BF16),
+            jax.ShapeDtypeStruct(cache.shape, BF16),
+        ),
+        in_specs=[pl.BlockSpec(memory_space=pl.ANY)] * 2,
+        out_specs=(pl.BlockSpec(memory_space=pl.ANY),) * 2,
+        scratch_shapes=[sem((2,))],
+    )(pltpu.with_memory_space_constraint(hid, pltpu.VMEM), pltpu.with_memory_space_constraint(cache, pltpu.VMEM))
     return (
         hid.reshape(1, micro, tok, width),
         cache.reshape(1, 2, micro, tok, width),

time: 46.7 us -> 46.1 us (0.987)
  local copies, waits for them, and re-layouts: 1.26 us -> 0 us
  Pallas kernels: 44 us -> 44.7 us
    unnamed x2 -> x0, local copies, waits for them, and re-layouts: 1.26 us -> none
    pallas_call x0 -> x1, Pallas kernels: none -> 0.68 us  [shards(): pl.pallas_call(store, out_shape=(jax.ShapeDtypeStruct(hid.shape, BF16), j...]
where the time goes in v3:
time: 46.1 us; the launch traced here: 46 us
  Pallas kernels  44.7 us (97%)
  between operations  1.29 us (3%)
    pallas_call x1, Pallas kernels, shards(): pl.pallas_call(functools.partial(kernel, (S, B, heads, hd, micro, tok)),...  44 us

profile of v3, /device:TPU:3, one launch (start us, length us, event | category | flops | bytes accessed | tf_op | source)
XLA Modules:
  0.0 46.0 jit_solution(11068841249488313041)
XLA Ops:
  1.3 44.0 %shard_map.104 = (bf16[32,768]{1,0:T(8,128)(2,1)S(1)}, bf16[2,32,768]{2,1,0:T(8,128)(2,1)S(1)}) custom-call(s32[1]{0:T(128)S(6)} %copy.11.text_len_in, s32[4]{0:T(128)} %patch_len_in.1, s32[2,4]{1,0:T(2,128)} %bitcast.14, bf16[32,768]{1,0:T(8,128)(2,1)} %bitcast.13, bf16[3,192,768]{2,1,0:T(8,128)(2,1)} %bitcast.10, f32[1,1536]{1,0:T(1,128)} %row_gain_in.1, ...), custom_call_target="tpu_custom_call" | custom-call | tf_op jit(solution)/shard_map/pallas_call | solution.py:523
  45.3 0.7 %shard_map.105 = (bf16[32,768]{1,0:T(8,128)(2,1)}, bf16[2,32,768]{2,1,0:T(8,128)(2,1)}) custom-call(bf16[32,768]{1,0:T(8,128)(2,1)S(1)} %get-tuple-element.6.hid, bf16[2,32,768]{2,1,0:T(8,128)(2,1)S(1)} %get-tuple-element.7.cache), custom_call_target="tpu_custom_call" | custom-call | tf_op jit(solution)/shard_map/pallas_call | solution.py:563

commit v4 on v3

--- a/solution.py
+++ b/solution.py
@@ -24,7 +24,7 @@
     text_len, patch_len, flags, row_gain, head_gain,
     X, X1, RES, XN, text_in, TN, W, R, PROJ, ST, TK, TV,
     hid_own, cache_own,
-    all_in, clear, taken, ls, xr, zs, zr, yr, rr, fs, one,
+    all_in, taken, ls, xr, zs, zr, yr, rr, fs, one,
 ):
     S, B, heads, hd, micro, tok = dims
     n = B // 2
@@ -279,14 +279,10 @@
         send_staying()
         with jax.named_scope("relay_done"):
             relay_done()
-        for k in range(2, n, 2):
-            pl.semaphore_signal(clear, inc=1, device_id=(s, in_half(k), h), device_id_type=MESH)
-        with jax.named_scope("clear"):
-            pl.semaphore_wait(clear, n // 2 - 1)
+        send_stale(near)
+        send_stale(far)
         send_crossing(near)
         send_crossing(far)
-        send_stale(near)
-        send_stale(far)
 
     def norm_states(values):
         XN[...] = rms(values.astype(F32), row_gain[...]).astype(BF16)
@@ -306,7 +302,7 @@
             norm_states(X[...].reshape(total, 2 * width))
             RES[...] = X[:, :, pl.ds(pl.multiple_of(h * width + j_own * hd, hd), hd)]
 
-    @pl.when(early & jnp.logical_not(owner))
+    @pl.when(early & (jnp.logical_not(owner) | (h == 1)))
     def _():
         with jax.named_scope("relayW1"):
             relay()
@@ -371,15 +367,13 @@
         )
 
     def push_cache():
-        for k in range(B):
-            t = ahead(k)
+        for t in range(B):
             push(cache_own.at[:, t], cache_out.at[:, :, cols_of(j_own)], cache_send, cache_recv, t)
 
     def push_hidden():
-        for k in range(B):
-            t = ahead(k)
+        for t in range(B):
             push(
-                hid_own.at[pl.ds(pl.multiple_of(t * rows, rows), rows), :],
+                hid_own.at[pl.ds(t * rows, rows), :],
                 hid_out.at[:, cols_of(j_own)], hid_send, hid_recv, t,
             )
 
@@ -439,7 +433,7 @@
             for k in range(0, B, 2):
                 remote(hid_own, col_block(j_own), zs.at[k // 2], zr.at[j_own], (s + 1, ahead(k), h)).start()
 
-        @pl.when(early)
+        @pl.when(early & (h == 0))
         def _():
             relay()
 
@@ -548,7 +542,7 @@
             pltpu.VMEM((text, hd), BF16),
             pltpu.VMEM((total, hd), BF16),
             pltpu.VMEM((2, B, rows, hd), BF16),
-            pltpu.SemaphoreType.REGULAR, pltpu.SemaphoreType.REGULAR, pltpu.SemaphoreType.REGULAR,
+            pltpu.SemaphoreType.REGULAR, pltpu.SemaphoreType.REGULAR,
             sem((5,)), sem((B,)), sem((n,)), sem((heads,)), sem((heads,)),
             sem((slots,)), sem((slots,)), sem((17,)),
         ],

time: 46.1 us -> 45.4 us (0.985)
  Pallas kernels: 44.7 us -> 43.9 us
    pallas_call x1, Pallas kernels: 44 us -> 43.2 us  [shards(): pl.pallas_call(functools.partial(kernel, (S, B, heads, hd, micro, tok)),...]
where the time goes in v4:
time: 45.4 us; the launch traced here: 45.2 us
  Pallas kernels  43.9 us (97%)
  between operations  1.29 us (3%)
    pallas_call x1, Pallas kernels, shards(): pl.pallas_call(functools.partial(kernel, (S, B, heads, hd, micro, tok)),...  43.2 us

profile of v4, /device:TPU:3, one launch (start us, length us, event | category | flops | bytes accessed | tf_op | source)
XLA Modules:
  0.0 45.2 jit_solution(6442604075651656961)
XLA Ops:
  1.3 43.2 %shard_map.104 = (bf16[32,768]{1,0:T(8,128)(2,1)S(1)}, bf16[2,32,768]{2,1,0:T(8,128)(2,1)S(1)}) custom-call(s32[1]{0:T(128)S(6)} %copy.11.text_len_in, s32[4]{0:T(128)} %patch_len_in.1, s32[2,4]{1,0:T(2,128)} %bitcast.14, bf16[32,768]{1,0:T(8,128)(2,1)} %bitcast.13, bf16[3,192,768]{2,1,0:T(8,128)(2,1)} %bitcast.10, f32[1,1536]{1,0:T(1,128)} %row_gain_in.1, ...), custom_call_target="tpu_custom_call" | custom-call | tf_op jit(solution)/shard_map/pallas_call | solution.py:517
  44.5 0.7 %shard_map.105 = (bf16[32,768]{1,0:T(8,128)(2,1)}, bf16[2,32,768]{2,1,0:T(8,128)(2,1)}) custom-call(bf16[32,768]{1,0:T(8,128)(2,1)S(1)} %get-tuple-element.6.hid, bf16[2,32,768]{2,1,0:T(8,128)(2,1)S(1)} %get-tuple-element.7.cache), custom_call_target="tpu_custom_call" | custom-call | tf_op jit(solution)/shard_map/pallas_call | solution.py:557

commit v5 on v4

--- a/solution.py
+++ b/solution.py
@@ -24,7 +24,7 @@
     text_len, patch_len, flags, row_gain, head_gain,
     X, X1, RES, XN, text_in, TN, W, R, PROJ, ST, TK, TV,
     hid_own, cache_own,
-    all_in, taken, ls, xr, zs, zr, yr, rr, fs, one,
+    all_in, clear, both, taken, ls, xr, zs, zr, yr, rr, fs, one,
 ):
     S, B, heads, hd, micro, tok = dims
     n = B // 2
@@ -148,23 +148,20 @@
 
     pl.semaphore_signal(all_in, inc=1, device_id=(s, across, h), device_id_type=MESH)
 
-    def other_side(c, t):
-        return 2 * t + lax.rem(c + off + 1, 2)
-
-    def central(c):
-        return lax.rem(c, n) // (n // 2) != c // n
+    def other_side(c, t, role):
+        return 2 * t + lax.rem(c + off + 1 + role, 2)
 
     def crosses(c, j):
         return (j < heads) & ((j + off) // n != c // n)
 
-    def detours(c, j):
-        return crosses(c, j) & (lax.rem(j + off + c, 2) == 1)
+    def detours(c, j, role):
+        return crosses(c, j) & (lax.rem(j + off + c + role, 2) == 1)
 
     def send_relayed():
         for t in range(slots):
-            j = other_side(b, t)
-
-            @pl.when(detours(b, j))
+            j = other_side(b, t, late)
+
+            @pl.when(detours(b, j, late))
             def _():
                 remote(w_cols(j), R.at[t], w_send, rr.at[t], (pair, jnp.where(late == 1, b, mate), h)).start()
 
@@ -172,7 +169,7 @@
         for k in range(heads):
             j = lax.rem(b + k, heads)
 
-            @pl.when(crosses(b, j) & jnp.logical_not(detours(b, j)) & which(j + off))
+            @pl.when(crosses(b, j) & jnp.logical_not(detours(b, j, late)) & which(j + off))
             def _():
                 remote(w_cols(j), w_rows(b), w_send, w_recv, (s, j + off, h)).start()
 
@@ -194,8 +191,8 @@
 
     def relayed(t):
         cb = jnp.where(late == 1, mate, b)
-        j = other_side(cb, t)
-        return detours(cb, j), remote(R.at[t], w_rows(cb), fs.at[t], w_recv, (pair, j + off, h))
+        j = other_side(cb, t, 1 - late)
+        return detours(cb, j, 1 - late), remote(R.at[t], w_rows(cb), fs.at[t], w_recv, (pair, j + off, h))
 
     def relay():
         for t in range(slots):
@@ -279,10 +276,17 @@
         send_staying()
         with jax.named_scope("relay_done"):
             relay_done()
+        for k in range(2, n, 2):
+            pl.semaphore_signal(clear, inc=1, device_id=(s, in_half(k), h), device_id_type=MESH)
+        with jax.named_scope("clear"):
+            pl.semaphore_wait(clear, n // 2 - 1)
+        pl.semaphore_signal(both, inc=1, device_id=core, device_id_type=MESH)
+        with jax.named_scope("both"):
+            pl.semaphore_wait(both, 1)
+        send_crossing(far)
+        send_crossing(near)
         send_stale(near)
         send_stale(far)
-        send_crossing(near)
-        send_crossing(far)
 
     def norm_states(values):
         XN[...] = rms(values.astype(F32), row_gain[...]).astype(BF16)
@@ -302,7 +306,7 @@
             norm_states(X[...].reshape(total, 2 * width))
             RES[...] = X[:, :, pl.ds(pl.multiple_of(h * width + j_own * hd, hd), hd)]
 
-    @pl.when(early & (jnp.logical_not(owner) | (h == 1)))
+    @pl.when(early & jnp.logical_not(owner))
     def _():
         with jax.named_scope("relayW1"):
             relay()
@@ -433,7 +437,7 @@
             for k in range(0, B, 2):
                 remote(hid_own, col_block(j_own), zs.at[k // 2], zr.at[j_own], (s + 1, ahead(k), h)).start()
 
-        @pl.when(early & (h == 0))
+        @pl.when(early)
         def _():
             relay()
 
@@ -543,6 +547,7 @@
             pltpu.VMEM((total, hd), BF16),
             pltpu.VMEM((2, B, rows, hd), BF16),
             pltpu.SemaphoreType.REGULAR, pltpu.SemaphoreType.REGULAR,
+            pltpu.SemaphoreType.REGULAR, pltpu.SemaphoreType.REGULAR,
             sem((5,)), sem((B,)), sem((n,)), sem((heads,)), sem((heads,)),
             sem((slots,)), sem((slots,)), sem((17,)),
         ],

time: 45.4 us -> 44.5 us (0.980)
  Pallas kernels: 43.9 us -> 42.9 us
    pallas_call x1, Pallas kernels: 43.2 us -> 42.2 us  [shards(): pl.pallas_call(functools.partial(kernel, (S, B, heads, hd, micro, tok)),...]
where the time goes in v5:
time: 44.5 us; the launch traced here: 44.2 us
  Pallas kernels  42.9 us (96%)
  between operations  1.29 us (3%)
    pallas_call x1, Pallas kernels, shards(): pl.pallas_call(functools.partial(kernel, (S, B, heads, hd, micro, tok)),...  42.2 us

profile of v5, /device:TPU:3, one launch (start us, length us, event | category | flops | bytes accessed | tf_op | source)
XLA Modules:
  0.0 44.2 jit_solution(16444153553117542182)
XLA Ops:
  1.3 42.2 %shard_map.104 = (bf16[32,768]{1,0:T(8,128)(2,1)S(1)}, bf16[2,32,768]{2,1,0:T(8,128)(2,1)S(1)}) custom-call(s32[1]{0:T(128)S(6)} %copy.11.text_len_in, s32[4]{0:T(128)} %patch_len_in.1, s32[2,4]{1,0:T(2,128)} %bitcast.14, bf16[32,768]{1,0:T(8,128)(2,1)} %bitcast.13, bf16[3,192,768]{2,1,0:T(8,128)(2,1)} %bitcast.10, f32[1,1536]{1,0:T(1,128)} %row_gain_in.1, ...), custom_call_target="tpu_custom_call" | custom-call | tf_op jit(solution)/shard_map/pallas_call | solution.py:521
  43.5 0.7 %shard_map.105 = (bf16[32,768]{1,0:T(8,128)(2,1)}, bf16[2,32,768]{2,1,0:T(8,128)(2,1)}) custom-call(bf16[32,768]{1,0:T(8,128)(2,1)S(1)} %get-tuple-element.6.hid, bf16[2,32,768]{2,1,0:T(8,128)(2,1)S(1)} %get-tuple-element.7.cache), custom_call_target="tpu_custom_call" | custom-call | tf_op jit(solution)/shard_map/pallas_call | solution.py:562

commit v6 on v5

--- a/solution.py
+++ b/solution.py
@@ -138,108 +138,108 @@
     def _():
         pltpu.make_async_copy(hid_in, row_block(b), x_own).start()
 
+
+    with jax.named_scope("barrier"):
+        pl.semaphore_wait(barrier, 2 * n + 2 + (linked.astype(jnp.int32) * n if S > 2 else 0))
+
+    pl.semaphore_signal(all_in, inc=1, device_id=(s, across, h), device_id_type=MESH)
+
+    def other_side(c, t, role):
+        return 2 * t + lax.rem(c + off + 1 + role, 2)
+
+    def crosses(c, j):
+        return (j < heads) & ((j + off) // n != c // n)
+
+    def detours(c, j, role):
+        return crosses(c, j) & (lax.rem(j + off + c + role, 2) == 1)
+
+    def send_relayed():
+        for t in range(slots):
+            j = other_side(b, t, late)
+
+            @pl.when(detours(b, j, late))
+            def _():
+                remote(w_cols(j), R.at[t], w_send, rr.at[t], (pair, jnp.where(late == 1, b, mate), h)).start()
+
+    def send_crossing(which):
+        for k in range(heads):
+            j = lax.rem(b + k, heads)
+
+            @pl.when(crosses(b, j) & jnp.logical_not(detours(b, j, late)) & which(j + off))
+            def _():
+                remote(w_cols(j), w_rows(b), w_send, w_recv, (s, j + off, h)).start()
+
+    def send_staying():
+        for k in range(heads):
+            j = lax.rem(b + k, heads)
+
+            @pl.when((j + off) // n == my_half)
+            def _():
+                push(w_cols(j), w_rows(b), w_send, w_recv, j + off)
+
+    def send_stale(which):
+        for k in range(heads):
+            j = lax.rem(b + k, heads)
+
+            @pl.when(which(j + off))
+            def _():
+                push(stale_in.at[:, :, cols_of(j)], ST.at[:, b], st_send, st_recv, j + off)
+
+    def relayed(t):
+        cb = jnp.where(late == 1, mate, b)
+        j = other_side(cb, t, 1 - late)
+        return detours(cb, j, 1 - late), remote(R.at[t], w_rows(cb), fs.at[t], w_recv, (pair, j + off, h))
+
+    def relay():
+        for t in range(slots):
+            used, onward = relayed(t)
+
+            @pl.when(used)
+            def _():
+                arrived(R.at[t], rr.at[t])
+                onward.start()
+
+    def relay_done():
+        for t in range(slots):
+            used, _ = relayed(t)
+
+            @pl.when(used)
+            def _():
+                sent(R.at[t], fs.at[t])
+
+    def send_states(which):
+        for k in range(2, B, 2):
+            @pl.when(which(nearest(k)))
+            def _():
+                remote(hid_in, row_block(b), x_send, xr.at[b], (s - 1, nearest(k), h)).start()
+
+    def block_to_core(c):
+        return remote(row_block(c), row_block(c), xc_send, xc_recv, core)
+
+    @pl.when(s == 1)
+    def _():
+        send_states(near)
+
+    @pl.when(early)
+    def _():
+        send_relayed()
+
+        @pl.when(s == 0)
+        def _():
+            pltpu.make_async_copy(hid_in, row_block(b), x_own).wait()
+            remote(row_block(b), row_block(b), xm_send, xr.at[b], (s, mate, h)).start()
+            block_to_core(b).start()
+
+        send_stale(near)
+
+        @pl.when(inner)
+        def _():
+            send_crossing(near)
+
     for load in loads:
         load.wait()
     text_copy.wait()
     TN[...] = rms(text_in[...].astype(F32), row_gain[...]).astype(BF16)
-
-    with jax.named_scope("barrier"):
-        pl.semaphore_wait(barrier, 2 * n + 2 + (linked.astype(jnp.int32) * n if S > 2 else 0))
-
-    pl.semaphore_signal(all_in, inc=1, device_id=(s, across, h), device_id_type=MESH)
-
-    def other_side(c, t, role):
-        return 2 * t + lax.rem(c + off + 1 + role, 2)
-
-    def crosses(c, j):
-        return (j < heads) & ((j + off) // n != c // n)
-
-    def detours(c, j, role):
-        return crosses(c, j) & (lax.rem(j + off + c + role, 2) == 1)
-
-    def send_relayed():
-        for t in range(slots):
-            j = other_side(b, t, late)
-
-            @pl.when(detours(b, j, late))
-            def _():
-                remote(w_cols(j), R.at[t], w_send, rr.at[t], (pair, jnp.where(late == 1, b, mate), h)).start()
-
-    def send_crossing(which):
-        for k in range(heads):
-            j = lax.rem(b + k, heads)
-
-            @pl.when(crosses(b, j) & jnp.logical_not(detours(b, j, late)) & which(j + off))
-            def _():
-                remote(w_cols(j), w_rows(b), w_send, w_recv, (s, j + off, h)).start()
-
-    def send_staying():
-        for k in range(heads):
-            j = lax.rem(b + k, heads)
-
-            @pl.when((j + off) // n == my_half)
-            def _():
-                push(w_cols(j), w_rows(b), w_send, w_recv, j + off)
-
-    def send_stale(which):
-        for k in range(heads):
-            j = lax.rem(b + k, heads)
-
-            @pl.when(which(j + off))
-            def _():
-                push(stale_in.at[:, :, cols_of(j)], ST.at[:, b], st_send, st_recv, j + off)
-
-    def relayed(t):
-        cb = jnp.where(late == 1, mate, b)
-        j = other_side(cb, t, 1 - late)
-        return detours(cb, j, 1 - late), remote(R.at[t], w_rows(cb), fs.at[t], w_recv, (pair, j + off, h))
-
-    def relay():
-        for t in range(slots):
-            used, onward = relayed(t)
-
-            @pl.when(used)
-            def _():
-                arrived(R.at[t], rr.at[t])
-                onward.start()
-
-    def relay_done():
-        for t in range(slots):
-            used, _ = relayed(t)
-
-            @pl.when(used)
-            def _():
-                sent(R.at[t], fs.at[t])
-
-    def send_states(which):
-        for k in range(2, B, 2):
-            @pl.when(which(nearest(k)))
-            def _():
-                remote(hid_in, row_block(b), x_send, xr.at[b], (s - 1, nearest(k), h)).start()
-
-    def block_to_core(c):
-        return remote(row_block(c), row_block(c), xc_send, xc_recv, core)
-
-    @pl.when(s == 1)
-    def _():
-        send_states(near)
-
-    @pl.when(early)
-    def _():
-        send_relayed()
-
-        @pl.when(s == 0)
-        def _():
-            pltpu.make_async_copy(hid_in, row_block(b), x_own).wait()
-            remote(row_block(b), row_block(b), xm_send, xr.at[b], (s, mate, h)).start()
-            block_to_core(b).start()
-
-        send_stale(near)
-
-        @pl.when(inner)
-        def _():
-            send_crossing(near)
-
     with jax.named_scope("all_in"):
         pl.semaphore_wait(all_in, 1)
 

time: 44.5 us -> 44 us (0.989)
  no operation moved by 1% of the time
where the time goes in v6:
time: 44 us; the launch traced here: 43.9 us
  Pallas kernels  42.6 us (97%)
  between operations  1.29 us (3%)
    pallas_call x1, Pallas kernels, shards(): pl.pallas_call(functools.partial(kernel, (S, B, heads, hd, micro, tok)),...  41.9 us

profile of v6, /device:TPU:3, one launch (start us, length us, event | category | flops | bytes accessed | tf_op | source)
XLA Modules:
  0.0 43.9 jit_solution(13773983124719815787)
XLA Ops:
  1.3 41.9 %shard_map.104 = (bf16[32,768]{1,0:T(8,128)(2,1)S(1)}, bf16[2,32,768]{2,1,0:T(8,128)(2,1)S(1)}) custom-call(s32[1]{0:T(128)S(6)} %copy.11.text_len_in, s32[4]{0:T(128)} %patch_len_in.1, s32[2,4]{1,0:T(2,128)} %bitcast.14, bf16[32,768]{1,0:T(8,128)(2,1)} %bitcast.13, bf16[3,192,768]{2,1,0:T(8,128)(2,1)} %bitcast.10, f32[1,1536]{1,0:T(1,128)} %row_gain_in.1, ...), custom_call_target="tpu_custom_call" | custom-call | tf_op jit(solution)/shard_map/pallas_call | solution.py:521
  43.2 0.7 %shard_map.105 = (bf16[32,768]{1,0:T(8,128)(2,1)}, bf16[2,32,768]{2,1,0:T(8,128)(2,1)}) custom-call(bf16[32,768]{1,0:T(8,128)(2,1)S(1)} %get-tuple-element.6.hid, bf16[2,32,768]{2,1,0:T(8,128)(2,1)S(1)} %get-tuple-element.7.cache), custom_call_target="tpu_custom_call" | custom-call | tf_op jit(solution)/shard_map/pallas_call | solution.py:562

commit v7 on v6

--- a/solution.py
+++ b/solution.py
@@ -236,10 +236,16 @@
         def _():
             send_crossing(near)
 
-    for load in loads:
-        load.wait()
-    text_copy.wait()
-    TN[...] = rms(text_in[...].astype(F32), row_gain[...]).astype(BF16)
+    def norm_text():
+        for load in loads:
+            load.wait()
+        text_copy.wait()
+        TN[...] = rms(text_in[...].astype(F32), row_gain[...]).astype(BF16)
+
+    @pl.when(early)
+    def _():
+        norm_text()
+
     with jax.named_scope("all_in"):
         pl.semaphore_wait(all_in, 1)
 
@@ -271,6 +277,7 @@
             send_states(far)
 
         send_relayed()
+        norm_text()
         with jax.named_scope("relay"):
             relay()
         send_staying()

time: 44 us -> 44 us (level)
  no operation moved by 1% of the time
where the time goes in v7:
time: 44 us; the launch traced here: 43.9 us
  Pallas kernels  42.6 us (97%)
  between operations  1.29 us (3%)
    pallas_call x1, Pallas kernels, shards(): pl.pallas_call(functools.partial(kernel, (S, B, heads, hd, micro, tok)),...  41.9 us

profile of v7, /device:TPU:3, one launch (start us, length us, event | category | flops | bytes accessed | tf_op | source)
XLA Modules:
  0.0 43.9 jit_solution(14725625761850912999)
XLA Ops:
  1.3 41.9 %shard_map.104 = (bf16[32,768]{1,0:T(8,128)(2,1)S(1)}, bf16[2,32,768]{2,1,0:T(8,128)(2,1)S(1)}) custom-call(s32[1]{0:T(128)S(6)} %copy.11.text_len_in, s32[4]{0:T(128)} %patch_len_in.1, s32[2,4]{1,0:T(2,128)} %bitcast.14, bf16[32,768]{1,0:T(8,128)(2,1)} %bitcast.13, bf16[3,192,768]{2,1,0:T(8,128)(2,1)} %bitcast.10, f32[1,1536]{1,0:T(1,128)} %row_gain_in.1, ...), custom_call_target="tpu_custom_call" | custom-call | tf_op jit(solution)/shard_map/pallas_call | solution.py:528
  43.2 0.7 %shard_map.105 = (bf16[32,768]{1,0:T(8,128)(2,1)}, bf16[2,32,768]{2,1,0:T(8,128)(2,1)}) custom-call(bf16[32,768]{1,0:T(8,128)(2,1)S(1)} %get-tuple-element.6.hid, bf16[2,32,768]{2,1,0:T(8,128)(2,1)S(1)} %get-tuple-element.7.cache), custom_call_target="tpu_custom_call" | custom-call | tf_op jit(solution)/shard_map/pallas_call | solution.py:569
